TPU v7x, 256 devices: a whole 4x4x8 slice. The times are simulated.
256 devices in a mesh: rows: 128 (over x, z, y), cols: 2 (over core).
Axes of the slice: x: 4, y: 4, z: 8, core: 2. Of those that a mesh axis runs over, the one named last changes fastest.
Arguments:
- points: float32 [8, 32768], P(None, ('cols', 'rows')), may hold values from -6 to 6
- targets: float32 [32768], P(('cols', 'rows')), may hold values from -6 to 6
- noise: float32 [64, 32768], P(None, ('cols', 'rows')), may hold values from -6 to 6
- omega: float32 [8, 2048], P(None, 'rows'), may hold values from -12 to 12
- phase: float32 [2048], P('rows'), may hold values from -3.140625 to 3.140625
- weights: float32 [2048, 64], P('rows'), may hold values from -6 to 6
Outputs:
- posterior: float32 [64, 32768], P(None, ('cols', 'rows'))
- residual: float32 [64, 32768], P(None, ('cols', 'rows'))
All inputs are finite; a program needn't handle non-finite values.
Results may differ from a plain program's by a relative error of at most 0.02.
Values may be sent and summed in bfloat16 or wider, within the bound.
A program may use at most 64 MiB of HBM per device.

v0:
```python
import functools
import math
import jax
import jax.numpy as jnp
from jax import lax
from jax.sharding import Mesh
from jax.sharding import PartitionSpec as P

ITERS = 2
ROWS = ("rows_0", "rows_1", "rows_2")
ROWS_COLS = ("rows_0", "rows_1", "rows_2", "cols")
COLS_ROWS = ("cols", "rows_0", "rows_1", "rows_2")


def turned_gather(arrays, axis, dims):
    turned = [jnp.moveaxis(a, dim, 0) for a, dim in zip(arrays, dims)]
    both = jnp.concatenate([t.reshape(len(t), -1) for t in turned], axis=1)
    whole, at, finished = (lax.all_gather(both, axis, axis=0, tiled=True), 0, [])
    for t, dim in zip(turned, dims):
        section = whole[:, at : at + t[0].size].reshape(-1, *t.shape[1:])
        finished.append(jnp.moveaxis(section, 0, dim))
        at += t[0].size
    return tuple(finished)


def over_axes(value, axes):
    return functools.reduce(lax.psum, axes, value)


def kernel_block(left, right):
    cross = lax.dot_general(
        left,
        right,
        (((0,), (0,)), ((), ())),
        precision=lax.Precision.HIGHEST,
        preferred_element_type=jnp.float32,
    )
    left_sq = jnp.sum(left * left, 0)
    right_sq = jnp.sum(right * right, 0)
    dist = left_sq[:, None] + right_sq[None, :] - 2.0 * cross
    return jnp.exp(-2.0 * dist).astype(jnp.bfloat16)


def body(points, targets, noise, omega, phase, weights):
    wide_omega, wide_phase, wide_weights = turned_gather((omega, phase, weights), ROWS, (1, 0, 0))
    features = jnp.cos(
        lax.dot_general(
            wide_omega,
            points,
            (((0,), (0,)), ((), ())),
            precision=lax.Precision.HIGHEST,
            preferred_element_type=jnp.float32,
        )
        + wide_phase[:, None]
    )
    prior = math.sqrt(2.0 / wide_weights.shape[0]) * lax.dot_general(
        wide_weights,
        features,
        (((0,), (0,)), ((), ())),
        precision=lax.Precision.HIGHEST,
        preferred_element_type=jnp.float32,
    )
    rhs = targets[None, :] - prior - 0.5 * noise
    columns = lax.all_gather(points, ROWS_COLS, axis=1, tiled=True)
    residual = rhs
    direction = rhs
    posterior = prior
    norm_now = over_axes(jnp.sum(residual * residual, 1), ROWS_COLS)
    for step in range(ITERS):
        low = direction.astype(jnp.bfloat16)
        kernel_part = jnp.dot(
            lax.all_gather(low, ROWS_COLS, axis=1, tiled=True),
            kernel_block(columns, points),
            preferred_element_type=jnp.float32,
        )
        image = kernel_part + 0.25 * direction
        curve, mixed, square = (
            over_axes(jnp.sum(direction * image, 1), ROWS_COLS),
            over_axes(jnp.sum(residual * image, 1), ROWS_COLS),
            over_axes(jnp.sum(image * image, 1), ROWS_COLS),
        )
        alpha = norm_now / curve
        norm_next = norm_now - 2.0 * alpha * mixed + alpha * alpha * square
        posterior = posterior + alpha[:, None] * kernel_part
        residual = residual - alpha[:, None] * image
        if step + 1 < ITERS:
            direction = residual + (norm_next / norm_now)[:, None] * direction
            norm_now = norm_next
    return (posterior, residual)


def solution(mesh):
    finer = Mesh(
        mesh.devices.reshape(4, 8, 4, mesh.shape["cols"]), ("rows_0", "rows_1", "rows_2", "cols")
    )
    in_specs = (
        P(None, COLS_ROWS),
        P(COLS_ROWS),
        P(None, COLS_ROWS),
        P(None, ROWS),
        P(ROWS),
        P(ROWS, None),
    )
    out_specs = (P(None, COLS_ROWS), P(None, COLS_ROWS))
    return jax.shard_map(body, mesh=finer, in_specs=in_specs, out_specs=out_specs, check_vma=False)
```

profile of v0, /device:TPU:1, one launch (start us, length us, event | category | flops | bytes accessed | tf_op | source)
XLA Modules:
  0.0 662.3 jit_solution(5400117945138848023)
XLA Ops:
  7.2 0.0 all-gather.6.cloned.1.call-start
  7.2 0.7 all-gather.6.cloned.1.call-update
  7.9 0.0 all-gather.4.cloned.1.call-start
  7.9 0.8 copy.10
  8.7 0.7 copy.11
  9.4 0.8 pad_maximum_fusion
  10.2 300.3 %all_gather.12 = f32[2048,73]{1,0:T(8,128)S(1)} all-gather(f32[16,73]{1,0:T(8,128)S(1)} %pad_maximum_fusion), channel_id=1, replica_groups=mesh['rows_0'=4,'rows_1'=8,'rows_2'=4,'cols'=2] {'rows_0','rows_1','rows..., dimensions={0}, use_global_device_ids=true | all-gather | bytes 602688 | tf_op jit(solution)/shard_map/all_gather | solution.py:18
  310.6 0.6 slice_reduce_fusion
  311.2 6.0 fusion.4
  317.2 3.6 fusion.9
  320.8 0.0 all-gather.4.cloned.1.call-update
  320.8 0.2 all-gather.8.cloned.1.call-start
  321.1 0.7 multiply_reduce_fusion.5
  321.8 0.0 all-gather.6.cloned.1.call-done
  321.8 1.5 multiply_reduce_fusion
  323.3 33.1 %fusion.3 = bf16[32768,128]{1,0:T(8,128)(2,1)} fusion(f32[8,32768]{1,0:T(8,128)} %all-gather.6.cloned.1.call-done, f32[8,128]{1,0:T(8,128)} %param.6, f32[128]{0:T(128)S(1)} %multiply_reduce_fusion.5, f32[32768]{0:T(1024)S(1)} %multiply_reduce_fusion), kind=kOutput, calls=%fused_computation.4 | convolution fusion | flops 423624704 | bytes 9572864 | tf_op jit(solution)/shard_map/dot_general | solution.py:31
  356.4 110.6 %all-gather.4.cloned.1.call-done = bf16[64,32768]{1,0:T(8,128)(2,1)} async-done(((bf16[64,128]{1,0:T(8,128)(2,1)}), bf16[64,32768]{1,0:T(8,128)(2,1)}) %all-gather.4.cloned.1.call-update) | async-done | bytes 4194320 | tf_op jit(solution)/shard_map/all_gather | solution.py:72
  467.0 6.4 multiply_reduce_fusion.3
  473.3 8.3 %all-reduce.2 = (f32[64]{0:T(128)S(1)}, f32[64]{0:T(128)S(1)}, f32[64]{0:T(128)S(1)}) all-reduce(f32[64]{0:T(128)S(1)} %get-tuple-element.3, f32[64]{0:T(128)S(1)} %get-tuple-element.4, f32[64]{0:T(128)S(1)} %get-tuple-element.2), channel_id=1, replica_groups=mesh['rows_0'=4,'rows_1'=8,'rows_2'=4,'cols'=2] {'rows_0'}, use_global_device_ids=true, to_apply=%region_13.0 | all-reduce | flops 192 | bytes 1536 | tf_op jit(solution)/shard_map/psum | solution.py:27
  481.7 13.1 %all-reduce = (f32[64]{0:T(128)S(1)}, f32[64]{0:T(128)S(1)}, f32[64]{0:T(128)S(1)}) all-reduce(f32[64]{0:T(128)S(1)} %get-tuple-element.11, f32[64]{0:T(128)S(1)} %get-tuple-element.12, f32[64]{0:T(128)S(1)} %get-tuple-element.13), channel_id=1, replica_groups=mesh['rows_0'=4,'rows_1'=8,'rows_2'=4,'cols'=2] {'rows_1'}, use_global_device_ids=true, to_apply=%region_14.0 | all-reduce | flops 192 | bytes 1536 | tf_op jit(solution)/shard_map/psum | solution.py:27
  494.8 8.4 %all-reduce.1 = (f32[64]{0:T(128)S(1)}, f32[64]{0:T(128)S(1)}, f32[64]{0:T(128)S(1)}) all-reduce(f32[64]{0:T(128)S(1)} %get-tuple-element.5, f32[64]{0:T(128)S(1)} %get-tuple-element.6, f32[64]{0:T(128)S(1)} %get-tuple-element.7), channel_id=1, replica_groups=mesh['rows_0'=4,'rows_1'=8,'rows_2'=4,'cols'=2] {'rows_2'}, use_global_device_ids=true, to_apply=%region_15.0 | all-reduce | flops 192 | bytes 1536 | tf_op jit(solution)/shard_map/psum | solution.py:27
  503.2 10.2 %all-reduce.3 = (f32[64]{0:T(128)S(1)}, f32[64]{0:T(128)S(1)}, f32[64]{0:T(128)S(1)}) all-reduce(f32[64]{0:T(128)S(1)} %get-tuple-element.8, f32[64]{0:T(128)S(1)} %get-tuple-element.9, f32[64]{0:T(128)S(1)} %get-tuple-element.10), channel_id=1, replica_groups=mesh['rows_0'=4,'rows_1'=8,'rows_2'=4,'cols'=2] {'cols'}, use_global_device_ids=true, to_apply=%region_16.0 | all-reduce | flops 192 | bytes 1536 | tf_op jit(solution)/shard_map/psum | solution.py:27
  513.4 0.7 fusion.7
  514.1 0.0 all-gather.8.cloned.1.call-update
  514.1 94.5 %all-gather.8.cloned.1.call-done = bf16[64,32768]{1,0:T(8,128)(2,1)} async-done(((bf16[64,128]{1,0:T(8,128)(2,1)}), bf16[64,32768]{1,0:T(8,128)(2,1)}) %all-gather.8.cloned.1.call-update) | async-done | bytes 4194320 | tf_op jit(solution)/shard_map/all_gather | solution.py:72
  608.7 6.3 multiply_reduce_fusion.1
  615.0 8.3 %psum.136 = f32[64]{0:T(128)S(1)} all-reduce(f32[64]{0:T(128)S(1)} %get-tuple-element.26), channel_id=1, replica_groups=mesh['rows_0'=4,'rows_1'=8,'rows_2'=4,'cols'=2] {'rows_0'}, use_global_device_ids=true, to_apply=%region_18.0 | all-reduce | flops 64 | bytes 512 | tf_op jit(solution)/shard_map/psum | solution.py:27
  623.4 13.1 %psum.137 = f32[64]{0:T(128)S(1)} all-reduce(f32[64]{0:T(128)S(1)} %psum.136), channel_id=1, replica_groups=mesh['rows_0'=4,'rows_1'=8,'rows_2'=4,'cols'=2] {'rows_1'}, use_global_device_ids=true, to_apply=%region_19.0 | all-reduce | flops 64 | bytes 512 | tf_op jit(solution)/shard_map/psum | solution.py:27
  636.5 8.4 %psum.138 = f32[64]{0:T(128)S(1)} all-reduce(f32[64]{0:T(128)S(1)} %psum.137), channel_id=1, replica_groups=mesh['rows_0'=4,'rows_1'=8,'rows_2'=4,'cols'=2] {'rows_2'}, use_global_device_ids=true, to_apply=%region_20.0 | all-reduce | flops 64 | bytes 512 | tf_op jit(solution)/shard_map/psum | solution.py:27
  644.9 10.2 %psum.139 = f32[64]{0:T(128)S(1)} all-reduce(f32[64]{0:T(128)S(1)} %psum.138), channel_id=1, replica_groups=mesh['rows_0'=4,'rows_1'=8,'rows_2'=4,'cols'=2] {'cols'}, use_global_device_ids=true, to_apply=%region_21.0 | all-reduce | flops 64 | bytes 512 | tf_op jit(solution)/shard_map/psum | solution.py:27
  655.1 0.7 multiply_subtract_fusion
  (2 shorter events, 0.0 us)
Async XLA Ops:
  7.2 314.6 %all-gather.6.cloned.1.call-start = ((), (), s32[]{:S(2)}) async-start(), calls=%async_computation.1 | async-start | bytes 1052672 | tf_op jit(solution)/shard_map/all_gather | solution.py:64
  7.9 459.1 %all-gather.4.cloned.1.call-start = ((), (), s32[]{:S(2)}) async-start(), calls=%async_computation | async-start | bytes 4210688 | tf_op jit(solution)/shard_map/all_gather | solution.py:72
  320.8 287.8 %all-gather.8.cloned.1.call-start = ((), (), s32[]{:S(2)}) async-start(), calls=%async_computation.2 | async-start | bytes 4210688 | tf_op jit(solution)/shard_map/all_gather | solution.py:72
Sparse Core Ops, SparseCore 0:
  11.7 107.1 all-gather.5
  321.0 145.9 all-gather.3
  514.2 94.3 all-gather.7
where the time goes:
time: 663 us; the launch traced here: 662 us
  blocking collectives  380 us (57%)
  waiting for transfers between devices  206 us (31%)
  matrix products  55.4 us (8%)
  between operations  13.8 us (2%)
    all_gather x1, blocking collectives, turned_gather(): lax.all_gather(both, axis, axis=0, tiled=True)  300 us
    all_gather x2, waiting for transfers between devices, body(): lax.all_gather(low, ROWS_COLS, axis=1, tiled=True)  205 us
    psum x8, blocking collectives, over_axes(): return functools.reduce(lax.psum, axes, value)  80.1 us
    dot_general x1, matrix products, kernel_block(): lax.dot_general(left, right, (((0,), (0,)), ((), ())), precision=lax.Prec...  33.1 us
  transfers between devices with their start and end apart: 3, of which 2 were waited for; matrix products, arithmetic and copies ran while one was open for 7% of the time, Pallas kernels for 0%

commit v1 on v0

--- a/solution.py
+++ b/solution.py
@@ -15,7 +15,16 @@
 def turned_gather(arrays, axis, dims):
     turned = [jnp.moveaxis(a, dim, 0) for a, dim in zip(arrays, dims)]
     both = jnp.concatenate([t.reshape(len(t), -1) for t in turned], axis=1)
-    whole, at, finished = (lax.all_gather(both, axis, axis=0, tiled=True), 0, [])
+    _work_racks = lambda x_in, peer_axis: jnp.concatenate(
+        lax.all_to_all(
+            jnp.stack([x_in for _ in range(lax.axis_size(peer_axis))]),
+            axis_name=peer_axis,
+            split_axis=0,
+            concat_axis=0,
+        ),
+        0,
+    )
+    whole, at, finished = (_work_racks(both, axis), 0, [])
     for t, dim in zip(turned, dims):
         section = whole[:, at : at + t[0].size].reshape(-1, *t.shape[1:])
         finished.append(jnp.moveaxis(section, 0, dim))

time: 663 us -> 419 us (0.63)
  blocking collectives: 380 us -> 124 us
  waiting for transfers between devices: 206 us -> 219 us
    all_gather x1 -> x0, blocking collectives: 300 us -> none  [turned_gather(): lax.all_gather(both, axis, axis=0, tiled=True)]
    all_gather x1, waiting for transfers between devices: 0.01 us -> 54.5 us  [body(): columns = lax.all_gather(points, ROWS_COLS, axis=1, tiled=True)]
    all_to_all x0 -> x1, blocking collectives: none -> 43.6 us  [turned_gather(): lax.all_to_all(jnp.stack([x_in for _ in range(lax.axis_size(peer_axis))])...]
    all_gather x2, waiting for transfers between devices: 205 us -> 164 us  [body(): lax.all_gather(low, ROWS_COLS, axis=1, tiled=True)]
  transfers between devices with their start and end apart: 3 -> 3, of which waited for: 2 -> 3; matrix products, arithmetic and copies ran while one was open for 7% -> 11% of each run, Pallas kernels for 0% -> 0%
where the time goes in v1:
time: 419 us; the launch traced here: 418 us
  waiting for transfers between devices  219 us (52%)
  blocking collectives  124 us (30%)
  matrix products  55.4 us (13%)
  between operations  13.8 us (3%)
    all_gather x2, waiting for transfers between devices, body(): lax.all_gather(low, ROWS_COLS, axis=1, tiled=True)  164 us
    psum x8, blocking collectives, over_axes(): return functools.reduce(lax.psum, axes, value)  80.1 us
    all_gather x1, waiting for transfers between devices, body(): columns = lax.all_gather(points, ROWS_COLS, axis=1, tiled=True)  54.5 us
    all_to_all x1, blocking collectives, turned_gather(): lax.all_to_all(jnp.stack([x_in for _ in range(lax.axis_size(peer_axis))])...  43.6 us
    dot_general x1, matrix products, kernel_block(): lax.dot_general(left, right, (((0,), (0,)), ((), ())), precision=lax.Prec...  33.1 us
    dot_general x2, matrix products, body(): jnp.dot(lax.all_gather(low, ROWS_COLS, axis=1, tiled=True), kernel_block(...  12.7 us
  transfers between devices with their start and end apart: 3, of which 3 were waited for; matrix products, arithmetic and copies ran while one was open for 11% of the time, Pallas kernels for 0%

profile of v1, /device:TPU:1, one launch (start us, length us, event | category | flops | bytes accessed | tf_op | source)
XLA Modules:
  0.0 418.0 jit_solution(11057418803850128560)
XLA Ops:
  7.2 0.0 copy-start
  7.2 0.0 all-gather.6.cloned.1.call-start
  7.2 0.7 all-gather.6.cloned.1.call-update
  7.9 0.0 all-gather.4.cloned.1.call-start
  8.0 0.8 copy.13
  8.7 0.7 copy.14
  9.4 0.8 pad_maximum_fusion
  10.2 0.1 stack.2
  10.3 43.6 %all_to_all.5 = f32[128,16,73]{2,1,0:T(8,128)S(1)} all-to-all(f32[128,16,73]{2,1,0:T(8,128)S(1)} %stack.2), channel_id=1, replica_groups=mesh['rows_0'=4,'rows_1'=8,'rows_2'=4,'cols'=2] {'rows_0','rows_1','rows..., dimensions={0} | all-to-all | bytes 1196032 | tf_op jit(solution)/shard_map/all_to_all | solution.py:19
  53.9 0.6 slice_reduce_fusion
  54.5 6.0 %fusion.4 = f32[2048,128]{1,0:T(8,128)S(1)} fusion(f32[8,128]{1,0:T(8,128)} %param.6, f32[2048,73]{1,0:T(8,128)S(1)} %bitcast.12, f32[2048]{0:T(1024)S(1)} %slice_reduce_fusion), kind=kOutput, calls=%fused_computation.6 | convolution fusion | flops 25427968 | bytes 1658880 | tf_op jit(solution)/shard_map/dot_general | solution.py:56
  60.5 3.6 fusion.9
  64.1 0.0 all-gather.4.cloned.1.call-update
  64.1 0.2 all-gather.8.cloned.1.call-start
  64.4 54.5 %all-gather.6.cloned.1.call-done = f32[8,32768]{1,0:T(8,128)} async-done(((f32[8,128]{1,0:T(8,128)}), f32[8,32768]{1,0:T(8,128)}) %all-gather.6.cloned.1.call-update) | async-done | bytes 1048592 | tf_op jit(solution)/shard_map/all_gather | solution.py:73
  118.9 1.5 multiply_reduce_fusion
  120.5 33.1 %fusion.3 = bf16[32768,128]{1,0:T(8,128)(2,1)} fusion(f32[8,32768]{1,0:T(8,128)} %all-gather.6.cloned.1.call-done, f32[8,128]{1,0:T(8,128)S(1)} %copy-done, f32[128]{0:T(128)S(1)} %multiply_reduce_fusion.5, f32[32768]{0:T(1024)S(1)} %multiply_reduce_fusion), kind=kOutput, calls=%fused_computation.4 | convolution fusion | flops 423624704 | bytes 9572864 | tf_op jit(solution)/shard_map/dot_general | solution.py:40
  153.6 69.1 %all-gather.4.cloned.1.call-done = bf16[64,32768]{1,0:T(8,128)(2,1)} async-done(((bf16[64,128]{1,0:T(8,128)(2,1)}), bf16[64,32768]{1,0:T(8,128)(2,1)}) %all-gather.4.cloned.1.call-update) | async-done | bytes 4194320 | tf_op jit(solution)/shard_map/all_gather | solution.py:81
  222.7 6.4 %multiply_reduce_fusion.3 = (f32[64]{0:T(128)S(1)}, f32[64]{0:T(128)S(1)}, f32[64]{0:T(128)S(1)}, f32[64,128]{1,0:T(8,128)S(1)}) fusion(f32[64,128]{1,0:T(8,128)S(1)} %get-tuple-element.21, bf16[64,32768]{1,0:T(8,128)(2,1)} %all-gather.4.cloned.1.call-done, bf16[32768,128]{1,0:T(8,128)(2,1)} %fusion.3), kind=kOutput, calls=%fused_computation.19 | convolution fusion | flops 536936256 | bytes 12649216 | tf_op jit(solution)/shard_map/dot_general | solution.py:80
  229.0 8.3 %all-reduce.2 = (f32[64]{0:T(128)S(1)}, f32[64]{0:T(128)S(1)}, f32[64]{0:T(128)S(1)}) all-reduce(f32[64]{0:T(128)S(1)} %get-tuple-element.3, f32[64]{0:T(128)S(1)} %get-tuple-element.4, f32[64]{0:T(128)S(1)} %get-tuple-element.2), channel_id=1, replica_groups=mesh['rows_0'=4,'rows_1'=8,'rows_2'=4,'cols'=2] {'rows_0'}, use_global_device_ids=true, to_apply=%region_13.0 | all-reduce | flops 192 | bytes 1536 | tf_op jit(solution)/shard_map/psum | solution.py:36
  237.4 13.1 %all-reduce = (f32[64]{0:T(128)S(1)}, f32[64]{0:T(128)S(1)}, f32[64]{0:T(128)S(1)}) all-reduce(f32[64]{0:T(128)S(1)} %get-tuple-element.11, f32[64]{0:T(128)S(1)} %get-tuple-element.12, f32[64]{0:T(128)S(1)} %get-tuple-element.13), channel_id=1, replica_groups=mesh['rows_0'=4,'rows_1'=8,'rows_2'=4,'cols'=2] {'rows_1'}, use_global_device_ids=true, to_apply=%region_14.0 | all-reduce | flops 192 | bytes 1536 | tf_op jit(solution)/shard_map/psum | solution.py:36
  250.5 8.4 %all-reduce.1 = (f32[64]{0:T(128)S(1)}, f32[64]{0:T(128)S(1)}, f32[64]{0:T(128)S(1)}) all-reduce(f32[64]{0:T(128)S(1)} %get-tuple-element.5, f32[64]{0:T(128)S(1)} %get-tuple-element.6, f32[64]{0:T(128)S(1)} %get-tuple-element.7), channel_id=1, replica_groups=mesh['rows_0'=4,'rows_1'=8,'rows_2'=4,'cols'=2] {'rows_2'}, use_global_device_ids=true, to_apply=%region_15.0 | all-reduce | flops 192 | bytes 1536 | tf_op jit(solution)/shard_map/psum | solution.py:36
  258.9 10.2 %all-reduce.3 = (f32[64]{0:T(128)S(1)}, f32[64]{0:T(128)S(1)}, f32[64]{0:T(128)S(1)}) all-reduce(f32[64]{0:T(128)S(1)} %get-tuple-element.8, f32[64]{0:T(128)S(1)} %get-tuple-element.9, f32[64]{0:T(128)S(1)} %get-tuple-element.10), channel_id=1, replica_groups=mesh['rows_0'=4,'rows_1'=8,'rows_2'=4,'cols'=2] {'cols'}, use_global_device_ids=true, to_apply=%region_16.0 | all-reduce | flops 192 | bytes 1536 | tf_op jit(solution)/shard_map/psum | solution.py:36
  269.1 0.7 fusion.7
  269.8 0.0 all-gather.8.cloned.1.call-update
  269.8 94.5 %all-gather.8.cloned.1.call-done = bf16[64,32768]{1,0:T(8,128)(2,1)} async-done(((bf16[64,128]{1,0:T(8,128)(2,1)}), bf16[64,32768]{1,0:T(8,128)(2,1)}) %all-gather.8.cloned.1.call-update) | async-done | bytes 4194320 | tf_op jit(solution)/shard_map/all_gather | solution.py:81
  364.4 6.3 %multiply_reduce_fusion.1 = (f32[64]{0:T(128)S(1)}, f32[64,128]{1,0:T(8,128)S(1)}) fusion(f32[64,128]{1,0:T(8,128)S(1)} %get-tuple-element.21, f32[64]{0:T(128)S(1)} %get-tuple-element.17, f32[64,128]{1,0:T(8,128)S(1)} %get-tuple-element.25, f32[64]{0:T(128)S(1)} %get-tuple-element.19, bf16[64,32768]{1,0:T(8,128)(2,1)} %all-gather.8.cloned.1.call-done, ...), kind=kOutput, calls=%fused_computation.14 | convolution fusion | flops 536952768 | bytes 12681984 | tf_op jit(solution)/shard_map/dot_general | solution.py:80
  370.7 8.3 %psum.136 = f32[64]{0:T(128)S(1)} all-reduce(f32[64]{0:T(128)S(1)} %get-tuple-element.26), channel_id=1, replica_groups=mesh['rows_0'=4,'rows_1'=8,'rows_2'=4,'cols'=2] {'rows_0'}, use_global_device_ids=true, to_apply=%region_18.0 | all-reduce | flops 64 | bytes 512 | tf_op jit(solution)/shard_map/psum | solution.py:36
  379.1 13.1 %psum.137 = f32[64]{0:T(128)S(1)} all-reduce(f32[64]{0:T(128)S(1)} %psum.136), channel_id=1, replica_groups=mesh['rows_0'=4,'rows_1'=8,'rows_2'=4,'cols'=2] {'rows_1'}, use_global_device_ids=true, to_apply=%region_19.0 | all-reduce | flops 64 | bytes 512 | tf_op jit(solution)/shard_map/psum | solution.py:36
  392.2 8.4 %psum.138 = f32[64]{0:T(128)S(1)} all-reduce(f32[64]{0:T(128)S(1)} %psum.137), channel_id=1, replica_groups=mesh['rows_0'=4,'rows_1'=8,'rows_2'=4,'cols'=2] {'rows_2'}, use_global_device_ids=true, to_apply=%region_20.0 | all-reduce | flops 64 | bytes 512 | tf_op jit(solution)/shard_map/psum | solution.py:36
  400.6 10.2 %psum.139 = f32[64]{0:T(128)S(1)} all-reduce(f32[64]{0:T(128)S(1)} %psum.138), channel_id=1, replica_groups=mesh['rows_0'=4,'rows_1'=8,'rows_2'=4,'cols'=2] {'cols'}, use_global_device_ids=true, to_apply=%region_21.0 | all-reduce | flops 64 | bytes 512 | tf_op jit(solution)/shard_map/psum | solution.py:36
  410.8 0.7 multiply_subtract_fusion
  (4 shorter events, 0.0 us)
Async XLA Ops:
  7.2 57.2 %copy-start = (f32[8,128]{1,0:T(8,128)S(1)}, f32[8,128]{1,0:T(8,128)}, u32[]{:S(2)}) copy-start(f32[8,128]{1,0:T(8,128)} %param.6) | copy-start | bytes 12292
  7.2 111.8 %all-gather.6.cloned.1.call-start = ((), (), s32[]{:S(2)}) async-start(), calls=%async_computation.2 | async-start | bytes 1052672 | tf_op jit(solution)/shard_map/all_gather | solution.py:73
  7.9 214.7 %all-gather.4.cloned.1.call-start = ((), (), s32[]{:S(2)}) async-start(), calls=%async_computation.1 | async-start | bytes 4210688 | tf_op jit(solution)/shard_map/all_gather | solution.py:81
  64.1 300.2 %all-gather.8.cloned.1.call-start = ((), (), s32[]{:S(2)}) async-start(), calls=%async_computation.3 | async-start | bytes 4210688 | tf_op jit(solution)/shard_map/all_gather | solution.py:81
Sparse Core Ops, SparseCore 0:
  11.7 107.1 all-gather.5
  123.3 99.3 all-gather.3
  269.9 94.3 all-gather.7
